TPU v7x, 32 devices: a whole 2x2x4 slice. The times are simulated.
32 devices in a mesh: grp: 2 (over x), ctx: 16 (over z, y, core).
Axes of the slice: x: 2, y: 2, z: 4, core: 2. Of those that a mesh axis runs over, the one named last changes fastest.
Arguments:
- cache_keys: bfloat16 [2048, 512], P(('grp', 'ctx')), parts along dimension 0, may hold values from -4 to 4
- cache_values: bfloat16 [2048, 512], P(('grp', 'ctx')), parts along dimension 0, may hold values from -4 to 4
- new_queries: bfloat16 [2048, 4096], P(('grp', 'ctx')), parts along dimension 0, may hold values from -600 to 600
- new_keys: bfloat16 [2048, 512], P(('grp', 'ctx')), parts along dimension 0, may hold values from -4 to 4
- new_values: bfloat16 [2048, 512], P(('grp', 'ctx')), parts along dimension 0, may hold values from -4 to 4
- cont_queries: bfloat16 [64, 4096], P(('grp', 'ctx')), parts along dimension 0, may hold values from -600 to 600
- suffix_keys: bfloat16 [64, 128, 512], P(('grp', 'ctx')), parts along dimension 0, may hold values from -4 to 4
- suffix_values: bfloat16 [64, 128, 512], P(('grp', 'ctx')), parts along dimension 0, may hold values from -4 to 4
- window_start: int32 [2], P('grp'), parts along dimension 0, may hold values from 0 to 255
- prefix_length: int32 [2], P('grp'), parts along dimension 0, may hold values from 512 to 1024
- suffix_length: int32 [64], P(('grp', 'ctx')), parts along dimension 0, may hold values from 2 to 128
Outputs:
- prompt_out: bfloat16 [2048, 4096], P(('grp', 'ctx')), parts along dimension 0
- cont_out: bfloat16 [64, 4096], P(('grp', 'ctx')), parts along dimension 0
There are 2 independent parts, one for each index of `grp`. A program takes and returns all parts, laid end to end along the dimension named above; each array names one. Nothing has to cross between parts.
All inputs are finite; a program needn't handle non-finite values.
Results may differ from a plain program's by a relative error of at most 0.009.
Values may be sent and summed in bfloat16 or wider, within the bound.
A program may use at most 192 MiB of HBM per device.

v0:
```python
import functools
import math

import jax
import jax.numpy as jnp
from jax import lax
from jax.experimental import pallas as pl
from jax.experimental.pallas import tpu as pltpu
from jax.sharding import PartitionSpec as P

KVH = 4
HD = 128
GROUP = 8
CORES = 2
PIECES = 4
EXTRA = 3
ORDER = (EXTRA, 0, 1, 2)
MESH = pl.DeviceIdType.MESH
SCALE2 = HD ** (-0.5) * math.log2(math.e)
HIDDEN = 1 << 30


def kernel(
    n_z,
    n_y,
    ck_ref,
    cv_ref,
    nq_ref,
    nk_ref,
    nv_ref,
    cq_ref,
    sk_ref,
    sv_ref,
    start_ref,
    prefix_ref,
    length_ref,
    out_ref,
    cont_ref,
    kv,
    q,
    sk,
    sv,
    rows16,
    limit,
    row_max,
    row_sum,
    acc,
    local_sem,
    query_sem,
    suffix_sem,
    recv_sem,
    pair_sem,
    send_sem,
):
    half = ck_ref.shape[0]
    prompt_rows = nq_ref.shape[0]
    conts = cq_ref.shape[0]
    suffix_rows = sk_ref.shape[1]
    many = GROUP * prompt_rows
    total = many + GROUP * conts
    me = lax.axis_index("ctx")
    core = me % CORES
    chip = me // CORES
    y = chip % n_y
    z = chip // n_y

    def device(zz, yy, cc):
        return (zz * n_y + yy) * CORES + cc

    own = []
    for p, ref in enumerate((ck_ref, nk_ref, cv_ref, nv_ref)):
        copy = pltpu.make_async_copy(
            ref, kv.at[me, p // 2, pl.ds((p % 2) * half, half)], local_sem.at[p]
        )
        copy.start()
        own.append(copy)
    for h in range(KVH):
        for g in range(GROUP):
            pltpu.make_async_copy(
                nq_ref.at[:, pl.ds((h * GROUP + g) * HD, HD)],
                q.at[h, pl.ds(g * prompt_rows, prompt_rows)],
                query_sem,
            ).start()
    suffix_copies = [
        pltpu.make_async_copy(sk_ref, sk, suffix_sem.at[0]),
        pltpu.make_async_copy(sv_ref, sv, suffix_sem.at[1]),
    ]
    for copy in suffix_copies:
        copy.start()

    barrier = pltpu.get_barrier_semaphore()

    def greet(target):
        pl.semaphore_signal(barrier, inc=1, device_id={"ctx": target}, device_id_type=MESH)

    greet(device(z, y, 1 - core))
    if n_y == 2:
        greet(device(z, 1 - y, core))

    @pl.when(z > 0)
    def _():
        greet(device(z - 1, y, core))

    @pl.when(z < n_z - 1)
    def _():
        greet(device(z + 1, y, core))

    line_neighbours = (z + n_z - 1) // n_z + (2 * n_z - 2 - z) // n_z
    pl.semaphore_wait(barrier, n_y + line_neighbours)

    def piece(source, p):
        return kv.at[source, p // 2, pl.ds((p % 2) * half, half)]

    def send(source, p, target, kind):
        ref = piece(source, p)
        sem = pair_sem.at[source] if kind == 2 else recv_sem.at[source, p]
        pltpu.make_async_remote_copy(
            src_ref=ref,
            dst_ref=ref,
            send_sem=send_sem.at[source, kind],
            recv_sem=sem,
            device_id={"ctx": target},
            device_id_type=MESH,
        ).start()

    def arrived(source, p):
        ref = piece(source, p)
        pltpu.make_async_copy(ref, ref, recv_sem.at[source, p]).wait()

    def pair_arrived(source):
        pltpu.make_async_copy(kv.at[source], kv.at[source], pair_sem.at[source]).wait()

    def sent(source, kind, pieces=PIECES):
        ref = kv.at[source]
        if pieces == 1:
            ref = piece(source, EXTRA)
        elif pieces < PIECES:
            ref = kv.at[source, :, pl.ds(0, pieces * half // 2)]
        pltpu.make_async_copy(ref, ref, send_sem.at[source, kind]).wait()

    def by_line(zs):
        return ((zs < z) & (zs < n_z - 2)) | ((zs > z) & (zs > 1))

    def not_by_line(zs):
        return ((zs < z) & (zs >= n_z - 2)) | ((zs > z) & (zs <= 1)) | (zs == z)

    partner = device(z, y, 1 - core)
    across = device(z, 1 - y, core)
    above = device(z + 1, y, core)
    below = device(z - 1, y, core)

    for p in ORDER:
        own[p].wait()

        @pl.when(z < n_z - 1)
        def _():
            send(me, p, above, 0)

        if n_y == 2:
            send(me, p, across, 4 if p == EXTRA else 1)

        @pl.when(z > 0)
        def _():
            send(me, p, below, 3)

        send(me, p, partner, 2)

    near = jnp.minimum(z, n_z - 1 - z)

    def z_at(t):
        if isinstance(t, int) and t == 0:
            return z
        step = (t + 1) // 2
        both = z + step * (1 - 2 * (t % 2))
        far = jnp.where(z + z < n_z - 1, t, n_z - 1 - t)
        return jnp.where(t <= 2 * near, both, far)

    row = lax.broadcasted_iota(jnp.int32, (total, HD), 0)
    limit[...] = jnp.where(row < many, me * prompt_rows + row % prompt_rows, HIDDEN - 1)
    row_max[...] = jnp.full_like(row_max, -1e30)
    row_sum[...] = jnp.zeros_like(row_sum)
    acc[...] = jnp.zeros_like(acc)
    for h in range(KVH):
        for g in range(GROUP):
            column = (h * GROUP + g) * HD
            rows16[h, g * conts : (g + 1) * conts, :] = cq_ref[:, column : column + HD].astype(
                jnp.float32
            )
    q[:, many:, :] = rows16[...].astype(jnp.bfloat16)

    for copy in suffix_copies:
        copy.wait()
    for h in range(KVH):
        keys = sk[:, :, h * HD : (h + 1) * HD].reshape(conts * suffix_rows, HD)
        values = sv[:, :, h * HD : (h + 1) * HD].reshape(conts * suffix_rows, HD)
        s = lax.dot_general(
            q[h, many:, :], keys, (((1,), (1,)), ((), ())), preferred_element_type=jnp.float32
        )
        who = lax.broadcasted_iota(jnp.int32, s.shape, 0) % conts
        column = lax.broadcasted_iota(jnp.int32, s.shape, 1)
        reach = jnp.zeros_like(who)
        for c in range(conts):
            reach = jnp.where(who == c, length_ref[c], reach)
        seen = (column // suffix_rows == who) & (column % suffix_rows < reach)
        s = jnp.where(seen, s * SCALE2, -1e30)
        top = jnp.max(s, axis=1, keepdims=True)
        w = jnp.exp2(s - top)
        row_max[h, many:, :] = jnp.broadcast_to(top, (GROUP * conts, HD))
        folded = w[:, :HD]
        for b in range(1, s.shape[1] // HD):
            folded = folded + w[:, b * HD : (b + 1) * HD]
        row_sum[h, many:, :] = folded
        acc[h, many:, :] = jnp.dot(
            w.astype(jnp.bfloat16), values, preferred_element_type=jnp.float32
        )

    span = CORES * 2 * half
    window_first = start_ref[0]
    prefix_last = prefix_ref[0]

    def places(chip_index):
        column = lax.broadcasted_iota(jnp.int32, (1, span), 1)
        within = column % (2 * half)
        position = (chip_index * CORES + column // (2 * half)) * half + within % half
        cached = jnp.where(
            (position >= window_first) & (position < prefix_last), -1, HIDDEN
        )
        return jnp.where(within < half, cached, position)

    def attend(h, chips, marks):
        cols = slice(h * HD, (h + 1) * HD)
        keys = [kv[pl.ds(c * CORES, CORES), 0, :, cols].reshape(span, HD) for c in chips]
        values = [kv[pl.ds(c * CORES, CORES), 1, :, cols].reshape(span, HD) for c in chips]
        keys = jnp.concatenate(keys, axis=0)
        values = jnp.concatenate(values, axis=0)
        mark = jnp.concatenate(marks, axis=1)
        count = span * len(chips)
        cut = (total // 2 + 15) // 16 * 16
        for lo, hi in ((0, cut), (cut, total)):
            s = lax.dot_general(
                q[h, lo:hi, :], keys, (((1,), (1,)), ((), ())), preferred_element_type=jnp.float32
            )
            bound = limit[lo:hi, :]
            blocks = []
            for b in range(count // HD):
                part = slice(b * HD, (b + 1) * HD)
                blocks.append(jnp.where(mark[:, part] <= bound, s[:, part] * SCALE2, -1e30))
            peak = functools.reduce(jnp.maximum, blocks)
            old = row_max[h, lo:hi, :]
            new = jnp.maximum(old, jnp.max(peak, axis=1, keepdims=True))
            alpha = jnp.exp2(old - new)
            w = [jnp.exp2(b - new) for b in blocks]
            row_max[h, lo:hi, :] = new
            row_sum[h, lo:hi, :] = row_sum[h, lo:hi, :] * alpha + functools.reduce(jnp.add, w)
            wb = jnp.concatenate([b.astype(jnp.bfloat16) for b in w], axis=1)
            acc[h, lo:hi, :] = acc[h, lo:hi, :] * alpha + jnp.dot(
                wb, values, preferred_element_type=jnp.float32
            )

    def onward(source, zs, p):
        @pl.when((zs < z) & (z < n_z - 1))
        def _():
            send(source, p, above, 0)

        @pl.when((zs > z) & (z > 0))
        def _():
            send(source, p, below, 0)

    def receive_z(zs, p):
        source = device(zs, y, core)
        arrived(source, p)
        onward(source, zs, p)
        if n_y == 2 and p == EXTRA:

            @pl.when(not_by_line(zs))
            def _():
                send(source, p, across, 4)

        elif n_y == 2:
            send(source, p, across, 1)
        send(source, p, partner, 2)

    def receive_extra(zs):
        @pl.when(by_line(zs))
        def _():
            source = device(zs, 1 - y, core)
            arrived(source, EXTRA)
            onward(source, zs, EXTRA)
            send(source, EXTRA, partner, 2)

    def receive_line(d, i):
        for zs, inside in ((z - d, z - d >= 0), (z + d, z + d < n_z)):

            @pl.when(inside)
            def _():
                receive_z(zs, ORDER[i])
                if n_y == 2 and i == PIECES - 1:
                    receive_extra(zs)

    def receive_y(zs, i):
        source = device(zs, 1 - y, core)
        p = ORDER[i]

        def take():
            arrived(source, p)
            send(source, p, partner, 2)

        if p == EXTRA:
            pl.when(not_by_line(zs))(take)
        else:
            take()

    def receive_pair(i):
        receive_y(z, i)
        if ORDER[i] == EXTRA:
            source = device(z, 1 - y, core)

            @pl.when(z < n_z - 2)
            def _():
                send(source, EXTRA, above, 0)

            @pl.when(z > 1)
            def _():
                send(source, EXTRA, below, 3)

    pltpu.make_async_copy(q.at[:, pl.ds(0, many)], q.at[:, pl.ds(0, many)], query_sem).wait()
    pair_arrived(partner)
    mark = places(chip)
    for h in range(KVH):
        attend(h, [chip], [mark])
        receive_line(1, h)
        if n_y == 2:
            receive_pair(h)

    def step(t, carry):
        zs, zb = z_at(t), z_at(t - 1)
        pair_arrived(device(zs, y, 1 - core))
        chips = [zs * n_y + y]
        if n_y == 2:
            pair_arrived(device(zb, 1 - y, 1 - core))
            chips.append(zb * n_y + 1 - y)
        marks = [places(c) for c in chips]
        for h in range(KVH):
            attend(h, chips, marks)

            @pl.when(t < n_z - 1)
            def _():
                receive_line(t + 1, h)

            if n_y == 2:
                receive_y(zs, h)
        return carry

    lax.fori_loop(1, n_z, step, 0)
    chips = []
    if n_y == 2:
        zb = z_at(jnp.int32(n_z - 1))
        pair_arrived(device(zb, 1 - y, 1 - core))
        chips = [zb * n_y + 1 - y]
    marks = [places(c) for c in chips]
    for h in range(KVH):
        if n_y == 2:
            attend(h, chips, marks)
        mixed = acc[h] / jnp.sum(row_sum[h], axis=1, keepdims=True)
        for g in range(GROUP):
            column = (h * GROUP + g) * HD
            out_ref[:, column : column + HD] = mixed[
                g * prompt_rows : (g + 1) * prompt_rows, :
            ].astype(jnp.bfloat16)
        rows16[h] = mixed[many:, :]
        for g in range(GROUP):
            column = (h * GROUP + g) * HD
            cont_ref[:, column : column + HD] = rows16[
                h, g * conts : (g + 1) * conts, :
            ].astype(jnp.bfloat16)

    @pl.when(z < n_z - 1)
    def _():
        sent(me, 0)

    @pl.when(z > 0)
    def _():
        sent(me, 3)

    sent(me, 2)
    if n_y == 2:
        pair = device(z, 1 - y, core)
        sent(me, 1, PIECES - 1)
        sent(me, 4, 1)

        @pl.when(z < n_z - 2)
        def _():
            sent(pair, 0, 1)

        @pl.when(z > 1)
        def _():
            sent(pair, 3, 1)

    def drain(zs, carry):
        source = device(zs, y, core)
        middle = ((zs < z) & (z < n_z - 1)) | ((zs > z) & (z > 0))

        @pl.when(middle)
        def _():
            sent(source, 0)

        @pl.when(zs != z)
        def _():
            if n_y == 2:
                sent(source, 1, PIECES - 1)
            sent(source, 2)

        if n_y == 2:
            other = device(zs, 1 - y, core)

            @pl.when((zs != z) & not_by_line(zs))
            def _():
                sent(source, 4, 1)

            @pl.when(middle & by_line(zs))
            def _():
                sent(other, 0, 1)

            sent(other, 2)
        return carry

    lax.fori_loop(0, n_z, drain, 0)


def line_shape(mesh):
    chips = mesh.shape["ctx"] // CORES
    place = mesh.axis_names.index("ctx")
    index = [0] * mesh.devices.ndim
    index[place] = slice(None)
    coords = [getattr(d, "coords", None) for d in mesh.devices[tuple(index)]]
    n_y = 1
    if all(c is not None for c in coords) and len({c[1] for c in coords}) == 2:
        n_y = 2
    return chips // n_y, n_y


def solution(mesh):
    n_z, n_y = line_shape(mesh)
    n_ctx = mesh.shape["ctx"]

    def body(ck, cv, nq, nk, nv, cq, sk, sv, ws, pfx, length):
        half, width = ck.shape
        rows = nq.shape[0]
        conts = cq.shape[0]
        total = GROUP * (rows + conts)
        anywhere = pl.BlockSpec(memory_space=pl.ANY)
        vmem = pl.BlockSpec(memory_space=pltpu.VMEM)
        smem = pl.BlockSpec(memory_space=pltpu.SMEM)
        return pl.pallas_call(
            functools.partial(kernel, n_z, n_y),
            out_shape=(
                pltpu.VMEM(nq.shape, jnp.bfloat16),
                pltpu.VMEM(cq.shape, jnp.bfloat16),
            ),
            in_specs=[anywhere] * 5 + [vmem] + [anywhere] * 2 + [smem] * 3,
            out_specs=(vmem, vmem),
            scratch_shapes=[
                pltpu.VMEM((n_ctx, 2, 2 * half, width), jnp.bfloat16),
                pltpu.VMEM((KVH, total, HD), jnp.bfloat16),
                pltpu.VMEM(sk.shape, jnp.bfloat16),
                pltpu.VMEM(sv.shape, jnp.bfloat16),
                pltpu.VMEM((KVH, GROUP * conts, HD), jnp.float32),
                pltpu.VMEM((total, HD), jnp.int32),
                pltpu.VMEM((KVH, total, HD), jnp.float32),
                pltpu.VMEM((KVH, total, HD), jnp.float32),
                pltpu.VMEM((KVH, total, HD), jnp.float32),
                pltpu.SemaphoreType.DMA((PIECES,)),
                pltpu.SemaphoreType.DMA,
                pltpu.SemaphoreType.DMA((2,)),
                pltpu.SemaphoreType.DMA((n_ctx, PIECES)),
                pltpu.SemaphoreType.DMA((n_ctx,)),
                pltpu.SemaphoreType.DMA((n_ctx, 5)),
            ],
            compiler_params=pltpu.CompilerParams(
                collective_id=0, has_side_effects=True, vmem_limit_bytes=60 * 1024 * 1024
            ),
        )(ck, cv, nq, nk, nv, cq, sk, sv, ws, pfx, length)

    part = P(("grp", "ctx"), None)
    part3 = P(("grp", "ctx"), None, None)
    in_specs = (part,) * 6 + (part3, part3, P("grp"), P("grp"), P(("grp", "ctx")))
    return jax.shard_map(
        body, mesh=mesh, in_specs=in_specs, out_specs=(part, part), check_vma=False
    )
```

profile of v0, /device:TPU:1, one launch (start us, length us, event | category | flops | bytes accessed | tf_op | source)
XLA Modules:
  0.0 37.5 jit_solution(14407797386631477560)
XLA Ops:
  1.9 34.2 %shard_map.122 = (bf16[64,4096]{1,0:T(8,128)(2,1)S(1)}, bf16[2,4096]{1,0:T(2,128)(2,1)S(1)}) custom-call(bf16[64,512]{1,0:T(8,128)(2,1)} %ck_ref.1, bf16[64,512]{1,0:T(8,128)(2,1)} %cv_ref.1, bf16[64,4096]{1,0:T(8,128)(2,1)} %nq_ref.1, bf16[64,512]{1,0:T(8,128)(2,1)} %nk_ref.1, bf16[64,512]{1,0:T(8,128)(2,1)} %nv_ref.1, bf16[2,4096]{1,0:T(2,128)(2,1)} %cq_ref.1, ...), custom_call_target="tpu_custom_call" | custom-call | tf_op jit(solution)/shard_map/pallas_call | solution.py:454
  36.1 0.8 %copy.15 = bf16[64,4096]{1,0:T(8,128)(2,1)} copy(bf16[64,4096]{1,0:T(8,128)(2,1)S(1)} %get-tuple-element.2) | data formatting | bytes 1048576
  36.9 0.6 %copy.16 = bf16[2,4096]{1,0:T(2,128)(2,1)} copy(bf16[2,4096]{1,0:T(2,128)(2,1)S(1)} %get-tuple-element.3) | data formatting | bytes 32768
where the time goes:
time: 37.8 us; the launch traced here: 37.5 us
  Pallas kernels  34.2 us (90%)
  between operations  1.93 us (5%)
  local copies, waits for them, and re-layouts  1.4 us (4%)
    pallas_call x1, Pallas kernels, body(): pl.pallas_call(functools.partial(kernel, n_z, n_y), out_shape=(pltpu.VMEM...  34.2 us
    unnamed x2, local copies, waits for them, and re-layouts  1.4 us

commit v1 on v0

--- a/solution.py
+++ b/solution.py
@@ -28,12 +28,12 @@
     nq_ref,
     nk_ref,
     nv_ref,
-    cq_ref,
+    cq_hbm,
     sk_ref,
     sv_ref,
-    start_ref,
-    prefix_ref,
-    length_ref,
+    start_hbm,
+    prefix_hbm,
+    length_hbm,
     out_ref,
     cont_ref,
     kv,
@@ -45,16 +45,21 @@
     row_max,
     row_sum,
     acc,
+    cq_ref,
+    start_ref,
+    prefix_ref,
+    length_ref,
     local_sem,
     query_sem,
     suffix_sem,
     recv_sem,
     pair_sem,
     send_sem,
+    small_sem,
 ):
     half = ck_ref.shape[0]
     prompt_rows = nq_ref.shape[0]
-    conts = cq_ref.shape[0]
+    conts = cq_hbm.shape[0]
     suffix_rows = sk_ref.shape[1]
     many = GROUP * prompt_rows
     total = many + GROUP * conts
@@ -85,7 +90,18 @@
         pltpu.make_async_copy(sk_ref, sk, suffix_sem.at[0]),
         pltpu.make_async_copy(sv_ref, sv, suffix_sem.at[1]),
     ]
-    for copy in suffix_copies:
+    small_copies = [
+        pltpu.make_async_copy(src, dst, small_sem.at[i])
+        for i, (src, dst) in enumerate(
+            (
+                (cq_hbm, cq_ref),
+                (start_hbm, start_ref),
+                (prefix_hbm, prefix_ref),
+                (length_hbm, length_ref),
+            )
+        )
+    ]
+    for copy in suffix_copies + small_copies:
         copy.start()
 
     barrier = pltpu.get_barrier_semaphore()
@@ -180,6 +196,8 @@
     row_max[...] = jnp.full_like(row_max, -1e30)
     row_sum[...] = jnp.zeros_like(row_sum)
     acc[...] = jnp.zeros_like(acc)
+    for copy in small_copies:
+        copy.wait()
     for h in range(KVH):
         for g in range(GROUP):
             column = (h * GROUP + g) * HD
@@ -427,6 +445,557 @@
     lax.fori_loop(0, n_z, drain, 0)
 
 
+HEADS = (0, 1, 2, 3)
+MOVED = None
+EXTRA_HEAD = 1
+
+
+def pack_rows(values):
+    lane = lax.broadcasted_iota(jnp.int32, (8, HD), 1)
+    tile = jnp.zeros((8, HD), jnp.float32)
+    for i in range(values.shape[0] // 8):
+        tile = jnp.where(lane == i, values[8 * i : 8 * i + 8, :], tile)
+    return tile
+
+
+def unpack_rows(tile, first, count):
+    lane = lax.broadcasted_iota(jnp.int32, (8, HD), 1)
+    blocks = [
+        jnp.max(jnp.where(lane == i, tile, -3e38), axis=1, keepdims=True)
+        for i in range(first // 8, (first + count) // 8)
+    ]
+    return jnp.concatenate(blocks, axis=0)
+
+
+def plane_kernel(
+    n_z,
+    ck_ref,
+    cv_ref,
+    nq_ref,
+    nk_ref,
+    nv_ref,
+    cq_hbm,
+    sk_ref,
+    sv_ref,
+    start_hbm,
+    prefix_hbm,
+    length_hbm,
+    out_ref,
+    cont_ref,
+    kv,
+    q,
+    sk,
+    sv,
+    rows16,
+    limit,
+    row_max,
+    row_sum,
+    acc,
+    cq,
+    far_cq,
+    part_out,
+    part_in,
+    lse_out,
+    lse_in,
+    start_ref,
+    prefix_ref,
+    length_ref,
+    local_sem,
+    query_sem,
+    suffix_sem,
+    small_sem,
+    recv_sem,
+    send_sem,
+    far_recv,
+    far_send,
+    part_recv,
+    part_send,
+):
+    n_y = 2
+    half = ck_ref.shape[0]
+    prompt_rows = nq_ref.shape[0]
+    conts = cq_hbm.shape[0]
+    suffix_rows = sk_ref.shape[1]
+    many = GROUP * prompt_rows
+    few = GROUP * conts
+    total = many + few
+    me = lax.axis_index("ctx")
+    core = me % CORES
+    chip = me // CORES
+    y = chip % n_y
+    z = chip // n_y
+    last = n_z - 1
+    lines = n_z - 2
+    plane = n_y * CORES
+    span = plane * half
+
+    def device(zz, yy, cc):
+        return (zz * n_y + yy) * CORES + cc
+
+    partner = device(z, y, 1 - core)
+    across = device(z, 1 - y, core)
+    above = device(z + 1, y, core)
+    below = device(z - 1, y, core)
+
+    for h in HEADS:
+        cols = pl.ds(h * HD, HD)
+        for kind, pair in enumerate(((ck_ref, cv_ref), (nk_ref, nv_ref))):
+            for i, ref in enumerate(pair):
+                pltpu.make_async_copy(ref.at[:, cols], kv.at[me, h, kind, i], local_sem.at[h]).start()
+    small = [
+        pltpu.make_async_copy(src, dst, small_sem.at[i])
+        for i, (src, dst) in enumerate(
+            (
+                (cq_hbm, cq),
+                (start_hbm, start_ref),
+                (prefix_hbm, prefix_ref),
+                (length_hbm, length_ref),
+            )
+        )
+    ]
+    for copy in small:
+        copy.start()
+    for h in HEADS:
+        for g in range(GROUP):
+            pltpu.make_async_copy(
+                nq_ref.at[:, pl.ds((h * GROUP + g) * HD, HD)],
+                q.at[h, pl.ds(g * prompt_rows, prompt_rows)],
+                query_sem,
+            ).start()
+    suffix_copies = [
+        pltpu.make_async_copy(sk_ref, sk, suffix_sem.at[0]),
+        pltpu.make_async_copy(sv_ref, sv, suffix_sem.at[1]),
+    ]
+    for copy in suffix_copies:
+        copy.start()
+
+    barrier = pltpu.get_barrier_semaphore()
+
+    def greet(target):
+        pl.semaphore_signal(barrier, inc=1, device_id={"ctx": target}, device_id_type=MESH)
+
+    greet(partner)
+    greet(across)
+
+    @pl.when(z > 0)
+    def _():
+        greet(below)
+
+    @pl.when(z < last)
+    def _():
+        greet(above)
+
+    line_neighbours = (z + n_z - 1) // n_z + (2 * n_z - 2 - z) // n_z
+    pl.semaphore_wait(barrier, n_y + line_neighbours)
+
+    def full(source, h):
+        return kv.at[source, h]
+
+    def cached(source, h):
+        return kv.at[source, h, 0]
+
+    def send(ref, source, h, target, kind):
+        pltpu.make_async_remote_copy(
+            src_ref=ref,
+            dst_ref=ref,
+            send_sem=send_sem.at[source, kind],
+            recv_sem=recv_sem.at[source, h],
+            device_id={"ctx": target},
+            device_id_type=MESH,
+        ).start()
+
+    def arrived(ref, source, h):
+        pltpu.make_async_copy(ref, ref, recv_sem.at[source, h]).wait()
+
+    def far_copy(zs, target):
+        return pltpu.make_async_remote_copy(
+            src_ref=far_cq.at[zs],
+            dst_ref=far_cq.at[zs],
+            send_sem=far_send.at[zs],
+            recv_sem=far_recv.at[zs],
+            device_id={"ctx": target},
+            device_id_type=MESH,
+        )
+
+    small[0].wait()
+
+    @pl.when(z < last)
+    def _():
+        pltpu.make_async_remote_copy(
+            src_ref=cq,
+            dst_ref=far_cq.at[z],
+            send_sem=far_send.at[z],
+            recv_sem=far_recv.at[z],
+            device_id={"ctx": above},
+            device_id_type=MESH,
+        ).start()
+
+    for h in HEADS:
+        pltpu.make_async_copy(full(me, h), full(me, h), local_sem.at[h]).wait()
+
+        @pl.when(z < last)
+        def _():
+            send(full(me, h), me, h, above, 0)
+
+        send(full(me, h), me, h, across, 1)
+
+        @pl.when(z > 0)
+        def _():
+            send(cached(me, h), me, h, below, 3)
+
+        send(full(me, h), me, h, partner, 2)
+
+    near = jnp.minimum(z, last - z)
+
+    def z_at(t):
+        step = (t + 1) // 2
+        both = z + step * (1 - 2 * (t % 2))
+        far = jnp.where(z + z < last, t, last - t)
+        return jnp.where(t <= 2 * near, both, far)
+
+    row = lax.broadcasted_iota(jnp.int32, (total, HD), 0)
+    limit[...] = jnp.where(row < many, (me % plane) * prompt_rows + row % prompt_rows, HIDDEN)
+    row_max[...] = jnp.full_like(row_max, -1e30)
+    row_sum[...] = jnp.zeros_like(row_sum)
+    acc[...] = jnp.zeros_like(acc)
+
+    def spread(rows):
+        for h in range(KVH):
+            for g in range(GROUP):
+                column = (h * GROUP + g) * HD
+                rows16[h, g * conts : (g + 1) * conts, :] = rows[:, column : column + HD].astype(
+                    jnp.float32
+                )
+
+    spread(cq)
+    q[:, many:, :] = rows16[...].astype(jnp.bfloat16)
+    for copy in small[1:]:
+        copy.wait()
+    for copy in suffix_copies:
+        copy.wait()
+    for h in range(KVH):
+        keys = sk[:, :, h * HD : (h + 1) * HD].reshape(conts * suffix_rows, HD)
+        values = sv[:, :, h * HD : (h + 1) * HD].reshape(conts * suffix_rows, HD)
+        s = lax.dot_general(
+            q[h, many:, :], keys, (((1,), (1,)), ((), ())), preferred_element_type=jnp.float32
+        )
+        who = lax.broadcasted_iota(jnp.int32, s.shape, 0) % conts
+        column = lax.broadcasted_iota(jnp.int32, s.shape, 1)
+        reach = jnp.zeros_like(who)
+        for c in range(conts):
+            reach = jnp.where(who == c, length_ref[c], reach)
+        seen = (column // suffix_rows == who) & (column % suffix_rows < reach)
+        s = jnp.where(seen, s * SCALE2, -1e30)
+        top = jnp.max(s, axis=1, keepdims=True)
+        w = jnp.exp2(s - top)
+        row_max[h, many:, :] = jnp.broadcast_to(top, (few, HD))
+        folded = w[:, :HD]
+        for b in range(1, s.shape[1] // HD):
+            folded = folded + w[:, b * HD : (b + 1) * HD]
+        row_sum[h, many:, :] = folded
+        acc[h, many:, :] = jnp.dot(
+            w.astype(jnp.bfloat16), values, preferred_element_type=jnp.float32
+        )
+
+    window_first = start_ref[0]
+    prefix_last = prefix_ref[0]
+
+    def cache_bias(zs):
+        position = zs * span + lax.broadcasted_iota(jnp.int32, (1, span), 1)
+        return jnp.where((position >= window_first) & (position < prefix_last), 0.0, -1e30)
+
+    def plane_rows(zs, h, kind, i):
+        return kv[pl.ds(zs * plane, plane), h, kind, i].reshape(span, HD)
+
+    def attend(h, zs, mode, bias):
+        keys = plane_rows(zs, h, 0, 0)
+        values = plane_rows(zs, h, 0, 1)
+        if mode != "cache":
+            keys = jnp.concatenate([keys, plane_rows(zs, h, 1, 0)], axis=0)
+            values = jnp.concatenate([values, plane_rows(zs, h, 1, 1)], axis=0)
+        cut = (total // 2 + 15) // 16 * 16
+        for lo, hi in ((0, cut), (cut, total)):
+            s = lax.dot_general(
+                q[h, lo:hi, :], keys, (((1,), (1,)), ((), ())), preferred_element_type=jnp.float32
+            )
+            blocks = []
+            for b in range(keys.shape[0] // HD):
+                part = s[:, b * HD : (b + 1) * HD] * SCALE2
+                if b < span // HD:
+                    part = part + bias[:, b * HD : (b + 1) * HD]
+                elif mode == "own":
+                    at = (b - span // HD) * HD + lax.broadcasted_iota(jnp.int32, (1, HD), 1)
+                    part = jnp.where(at <= limit[lo:hi, :], part, -1e30)
+                blocks.append(part)
+            peak = functools.reduce(jnp.maximum, blocks)
+            old = row_max[h, lo:hi, :]
+            new = jnp.maximum(old, jnp.max(peak, axis=1, keepdims=True))
+            alpha = jnp.exp2(old - new)
+            w = [jnp.exp2(b - new) for b in blocks]
+            row_max[h, lo:hi, :] = new
+            row_sum[h, lo:hi, :] = row_sum[h, lo:hi, :] * alpha + functools.reduce(jnp.add, w)
+            wb = jnp.concatenate([b.astype(jnp.bfloat16) for b in w], axis=1)
+            acc[h, lo:hi, :] = acc[h, lo:hi, :] * alpha + jnp.dot(
+                wb, values, preferred_element_type=jnp.float32
+            )
+
+    def foreign(zs):
+        spread(far_cq.at[zs])
+        sums = []
+        for h in range(KVH):
+            s = lax.dot_general(
+                rows16[h].astype(jnp.bfloat16),
+                plane_rows(z, h, 1, 0),
+                (((1,), (1,)), ((), ())),
+                preferred_element_type=jnp.float32,
+            )
+            s = s * SCALE2
+            top = jnp.max(s, axis=1, keepdims=True)
+            w = jnp.exp2(s - top)
+            under = jnp.sum(w, axis=1, keepdims=True)
+            mixed = jnp.dot(
+                w.astype(jnp.bfloat16), plane_rows(z, h, 1, 1), preferred_element_type=jnp.float32
+            )
+            part_out[zs, h * few : (h + 1) * few, :] = mixed / under
+            sums.append(jnp.broadcast_to(top + jnp.log2(under), (few, HD)))
+        lse_out[zs] = pack_rows(jnp.concatenate(sums, axis=0))
+
+    def part_copies(zs):
+        return [
+            pltpu.make_async_remote_copy(
+                src_ref=src.at[zs],
+                dst_ref=dst.at[z],
+                send_sem=part_send.at[zs, i],
+                recv_sem=part_recv.at[z, i],
+                device_id={"ctx": device(zs, y, core)},
+                device_id_type=MESH,
+            )
+            for i, (src, dst) in enumerate(((part_out, part_in), (lse_out, lse_in)))
+        ]
+
+    def merge(zs):
+        for i, ref in enumerate((part_in, lse_in)):
+            pltpu.make_async_copy(ref.at[zs], ref.at[zs], part_recv.at[zs, i]).wait()
+        tile = lse_in[zs]
+        lane = lax.broadcasted_iota(jnp.int32, (few, HD), 1)
+        for h in range(KVH):
+            level = unpack_rows(tile, h * few, few)
+            old = row_max[h, many:, :]
+            new = jnp.maximum(old, level)
+            alpha = jnp.exp2(old - new)
+            beta = jnp.exp2(level - new)
+            row_max[h, many:, :] = new
+            row_sum[h, many:, :] = row_sum[h, many:, :] * alpha + jnp.where(lane == 0, beta, 0.0)
+            acc[h, many:, :] = (
+                acc[h, many:, :] * alpha + part_in[zs, h * few : (h + 1) * few, :] * beta
+            )
+
+    def receive_line(d, i):
+        h = HEADS[i]
+        low, high = z - d, z + d
+
+        @pl.when(low >= 0)
+        def _():
+            source = device(low, y, core)
+            ref = full(source, h)
+            if i == 0:
+                pltpu.make_async_copy(far_cq.at[low], far_cq.at[low], far_recv.at[low]).wait()
+
+                @pl.when(z < last)
+                def _():
+                    far_copy(low, above).start()
+
+            arrived(ref, source, h)
+
+            @pl.when(z < last)
+            def _():
+                send(ref, source, h, above, 0)
+
+            if h == EXTRA_HEAD:
+
+                @pl.when(low >= lines)
+                def _():
+                    send(ref, source, h, across, 1)
+
+            else:
+                send(ref, source, h, across, 1)
+            send(ref, source, h, partner, 2)
+            if i == KVH - 1:
+
+                @pl.when(low < lines)
+                def _():
+                    other = device(low, 1 - y, core)
+                    extra = full(other, EXTRA_HEAD)
+                    arrived(extra, other, EXTRA_HEAD)
+
+                    @pl.when(z < last)
+                    def _():
+                        send(extra, other, EXTRA_HEAD, above, 0)
+
+                    send(extra, other, EXTRA_HEAD, partner, 2)
+
+        @pl.when(high < n_z)
+        def _():
+            source = device(high, y, core)
+            ref = cached(source, h)
+            arrived(ref, source, h)
+
+            @pl.when(z > 0)
+            def _():
+                send(ref, source, h, below, 0)
+
+            send(ref, source, h, across, 1)
+            send(ref, source, h, partner, 2)
+
+    def receive_y(zs, i):
+        h = HEADS[i]
+        source = device(zs, 1 - y, core)
+
+        def take(ref):
+            arrived(ref, source, h)
+            send(ref, source, h, partner, 2)
+
+        if h == EXTRA_HEAD:
+            pl.when((zs <= z) & ((zs == z) | (zs >= lines)))(lambda: take(full(source, h)))
+        else:
+            pl.when(zs <= z)(lambda: take(full(source, h)))
+        pl.when(zs > z)(lambda: take(cached(source, h)))
+
+    def receive_own(i):
+        h = HEADS[i]
+        arrived(full(across, h), across, h)
+        send(full(across, h), across, h, partner, 2)
+        if h == EXTRA_HEAD:
+
+            @pl.when((z < last) & (z < lines))
+            def _():
+                send(full(across, h), across, h, above, 0)
+
+    def pair_arrived(zs, i):
+        h = HEADS[i]
+        for yy in (y, 1 - y):
+            source = device(zs, yy, 1 - core)
+            pl.when(zs <= z)(lambda source=source: arrived(full(source, h), source, h))
+            pl.when(zs > z)(lambda source=source: arrived(cached(source, h), source, h))
+
+    pltpu.make_async_copy(
+        q.at[pl.ds(0, KVH), pl.ds(0, many)], q.at[pl.ds(0, KVH), pl.ds(0, many)], query_sem
+    ).wait()
+    receive_own(0)
+    receive_own(1)
+    bias = cache_bias(z)
+    for i, h in enumerate(HEADS):
+        for yy in (y, 1 - y):
+            source = device(z, yy, 1 - core)
+            arrived(full(source, h), source, h)
+        attend(h, z, "own", bias)
+        receive_line(1, i)
+        if i + 2 < KVH:
+            receive_own(i + 2)
+
+    @pl.when(z > 0)
+    def _():
+        foreign(z - 1)
+
+    def give(zs):
+        for copy in part_copies(zs):
+            copy.start()
+
+    def step(t, carry):
+        zs = z_at(t)
+        bias = cache_bias(zs)
+        receive_y(zs, 0)
+        for i, h in enumerate(HEADS):
+            if i + 1 < KVH:
+                receive_y(zs, i + 1)
+            pair_arrived(zs, i)
+            pl.when(zs < z)(lambda: attend(h, zs, "all", bias))
+            pl.when(zs > z)(lambda: attend(h, zs, "cache", bias))
+
+            if i == 0:
+                pl.when((t == 1) & (z > 0))(lambda: give(z - 1))
+
+            @pl.when(t < last)
+            def _():
+                receive_line(t + 1, i)
+                if i < 2:
+                    pl.when(z - t - 1 >= 0)(lambda: (foreign, give)[i](z - t - 1))
+
+        return carry
+
+    lax.fori_loop(1, n_z, step, 0)
+
+    def collect(zs, carry):
+        merge(zs)
+        return carry
+
+    lax.fori_loop(z + 1, n_z, collect, 0)
+    for h in range(KVH):
+        mixed = acc[h] / jnp.sum(row_sum[h], axis=1, keepdims=True)
+        for g in range(GROUP):
+            column = (h * GROUP + g) * HD
+            out_ref[:, column : column + HD] = mixed[
+                g * prompt_rows : (g + 1) * prompt_rows, :
+            ].astype(jnp.bfloat16)
+        rows16[h] = mixed[many:, :]
+        for g in range(GROUP):
+            column = (h * GROUP + g) * HD
+            cont_ref[:, column : column + HD] = rows16[
+                h, g * conts : (g + 1) * conts, :
+            ].astype(jnp.bfloat16)
+
+    def sent(source, kind, count, cache_only=False):
+        ref = kv.at[source, pl.ds(0, count)]
+        if cache_only:
+            ref = kv.at[source, pl.ds(0, count), 0]
+        pltpu.make_async_copy(ref, ref, send_sem.at[source, kind]).wait()
+
+    @pl.when(z < last)
+    def _():
+        sent(me, 0, KVH)
+        pltpu.make_async_copy(cq, cq, far_send.at[z]).wait()
+
+    @pl.when(z > 0)
+    def _():
+        sent(me, 3, KVH, True)
+
+    sent(me, 1, KVH)
+    sent(me, 2, KVH)
+
+    def drain(zs, carry):
+        source = device(zs, y, core)
+        other = device(zs, 1 - y, core)
+
+        @pl.when(zs < z)
+        def _():
+            @pl.when(z < last)
+            def _():
+                sent(source, 0, KVH)
+                pltpu.make_async_copy(far_cq.at[zs], far_cq.at[zs], far_send.at[zs]).wait()
+
+            pl.when(zs < lines)(lambda: sent(source, 1, KVH - 1))
+            pl.when(zs >= lines)(lambda: sent(source, 1, KVH))
+            sent(source, 2, KVH)
+            for copy in part_copies(zs):
+                copy.wait_send()
+
+        @pl.when(zs > z)
+        def _():
+            pl.when(z > 0)(lambda: sent(source, 0, KVH, True))
+            sent(source, 1, KVH, True)
+            sent(source, 2, KVH, True)
+            sent(other, 2, KVH, True)
+
+        @pl.when(zs <= z)
+        def _():
+            sent(other, 2, KVH)
+            pl.when((z < last) & (zs < lines))(lambda: sent(other, 0, 1))
+
+        return carry
+
+    lax.fori_loop(0, n_z, drain, 0)
+
+
 def line_shape(mesh):
     chips = mesh.shape["ctx"] // CORES
     place = mesh.axis_names.index("ctx")
@@ -443,6 +1012,58 @@
     n_z, n_y = line_shape(mesh)
     n_ctx = mesh.shape["ctx"]
 
+    def plane_body(ck, cv, nq, nk, nv, cq, sk, sv, ws, pfx, length):
+        half = ck.shape[0]
+        few = GROUP * cq.shape[0]
+        total = GROUP * nq.shape[0] + few
+        anywhere = pl.BlockSpec(memory_space=pl.ANY)
+        vmem = pl.BlockSpec(memory_space=pltpu.VMEM)
+        state = pltpu.VMEM((KVH, total, HD), jnp.float32)
+        part = pltpu.VMEM((n_z, KVH * few, HD), jnp.float32)
+        levels = pltpu.VMEM((n_z, 8, HD), jnp.float32)
+        return pl.pallas_call(
+            functools.partial(plane_kernel, n_z),
+            out_shape=(
+                pltpu.VMEM(nq.shape, jnp.bfloat16),
+                pltpu.VMEM(cq.shape, jnp.bfloat16),
+            ),
+            in_specs=[anywhere] * 11,
+            out_specs=(vmem, vmem),
+            scratch_shapes=[
+                pltpu.VMEM((n_ctx, KVH, 2, 2, half, HD), jnp.bfloat16),
+                pltpu.VMEM((KVH, total, HD), jnp.bfloat16),
+                pltpu.VMEM(sk.shape, jnp.bfloat16),
+                pltpu.VMEM(sv.shape, jnp.bfloat16),
+                pltpu.VMEM((KVH, few, HD), jnp.float32),
+                pltpu.VMEM((total, HD), jnp.int32),
+                state,
+                state,
+                state,
+                pltpu.VMEM(cq.shape, jnp.bfloat16),
+                pltpu.VMEM((n_z,) + cq.shape, jnp.bfloat16),
+                part,
+                part,
+                levels,
+                levels,
+                pltpu.SMEM(ws.shape, jnp.int32),
+                pltpu.SMEM(pfx.shape, jnp.int32),
+                pltpu.SMEM(length.shape, jnp.int32),
+                pltpu.SemaphoreType.DMA((KVH,)),
+                pltpu.SemaphoreType.DMA,
+                pltpu.SemaphoreType.DMA((2,)),
+                pltpu.SemaphoreType.DMA((4,)),
+                pltpu.SemaphoreType.DMA((n_ctx, KVH)),
+                pltpu.SemaphoreType.DMA((n_ctx, 4)),
+                pltpu.SemaphoreType.DMA((n_z,)),
+                pltpu.SemaphoreType.DMA((n_z,)),
+                pltpu.SemaphoreType.DMA((n_z, 2)),
+                pltpu.SemaphoreType.DMA((n_z, 2)),
+            ],
+            compiler_params=pltpu.CompilerParams(
+                collective_id=0, has_side_effects=True, vmem_limit_bytes=60 * 1024 * 1024
+            ),
+        )(ck, cv, nq, nk, nv, cq, sk, sv, ws, pfx, length)
+
     def body(ck, cv, nq, nk, nv, cq, sk, sv, ws, pfx, length):
         half, width = ck.shape
         rows = nq.shape[0]
@@ -450,14 +1071,13 @@
         total = GROUP * (rows + conts)
         anywhere = pl.BlockSpec(memory_space=pl.ANY)
         vmem = pl.BlockSpec(memory_space=pltpu.VMEM)
-        smem = pl.BlockSpec(memory_space=pltpu.SMEM)
         return pl.pallas_call(
             functools.partial(kernel, n_z, n_y),
             out_shape=(
                 pltpu.VMEM(nq.shape, jnp.bfloat16),
                 pltpu.VMEM(cq.shape, jnp.bfloat16),
             ),
-            in_specs=[anywhere] * 5 + [vmem] + [anywhere] * 2 + [smem] * 3,
+            in_specs=[anywhere] * 11,
             out_specs=(vmem, vmem),
             scratch_shapes=[
                 pltpu.VMEM((n_ctx, 2, 2 * half, width), jnp.bfloat16),
@@ -469,12 +1089,17 @@
                 pltpu.VMEM((KVH, total, HD), jnp.float32),
                 pltpu.VMEM((KVH, total, HD), jnp.float32),
                 pltpu.VMEM((KVH, total, HD), jnp.float32),
+                pltpu.VMEM(cq.shape, jnp.bfloat16),
+                pltpu.SMEM(ws.shape, jnp.int32),
+                pltpu.SMEM(pfx.shape, jnp.int32),
+                pltpu.SMEM(length.shape, jnp.int32),
                 pltpu.SemaphoreType.DMA((PIECES,)),
                 pltpu.SemaphoreType.DMA,
                 pltpu.SemaphoreType.DMA((2,)),
                 pltpu.SemaphoreType.DMA((n_ctx, PIECES)),
                 pltpu.SemaphoreType.DMA((n_ctx,)),
                 pltpu.SemaphoreType.DMA((n_ctx, 5)),
+                pltpu.SemaphoreType.DMA((4,)),
             ],
             compiler_params=pltpu.CompilerParams(
                 collective_id=0, has_side_effects=True, vmem_limit_bytes=60 * 1024 * 1024
@@ -485,5 +1110,6 @@
     part3 = P(("grp", "ctx"), None, None)
     in_specs = (part,) * 6 + (part3, part3, P("grp"), P("grp"), P(("grp", "ctx")))
     return jax.shard_map(
-        body, mesh=mesh, in_specs=in_specs, out_specs=(part, part), check_vma=False
+        plane_body if n_y == 2 and n_z > 2 else body,
+        mesh=mesh, in_specs=in_specs, out_specs=(part, part), check_vma=False
     )

time: 37.8 us -> 35 us (0.926)
  the two profiles are of different devices: /device:TPU:1 before, /device:TPU:25 now
where the time goes in v1:
time: 35 us; the launch traced here: 34.8 us
  Pallas kernels  31.5 us (90%)
  between operations  1.93 us (6%)
  local copies, waits for them, and re-layouts  1.4 us (4%)
    pallas_call x1, Pallas kernels, plane_body(): pl.pallas_call(functools.partial(plane_kernel, n_z), out_shape=(pltpu.VME...  31.5 us
    unnamed x2, local copies, waits for them, and re-layouts  1.4 us

profile of v1, /device:TPU:25, one launch (start us, length us, event | category | flops | bytes accessed | tf_op | source)
XLA Modules:
  0.0 34.8 jit_solution(8444120327923085894)
XLA Ops:
  1.9 31.5 %shard_map.122 = (bf16[64,4096]{1,0:T(8,128)(2,1)S(1)}, bf16[2,4096]{1,0:T(2,128)(2,1)S(1)}) custom-call(bf16[64,512]{1,0:T(8,128)(2,1)} %ck_ref.1, bf16[64,512]{1,0:T(8,128)(2,1)} %cv_ref.1, bf16[64,4096]{1,0:T(8,128)(2,1)} %nq_ref.1, bf16[64,512]{1,0:T(8,128)(2,1)} %nk_ref.1, bf16[64,512]{1,0:T(8,128)(2,1)} %nv_ref.1, bf16[2,4096]{1,0:T(2,128)(2,1)} %cq_hbm.1, ...), custom_call_target="tpu_custom_call" | custom-call | tf_op jit(solution)/shard_map/pallas_call | solution.py:1024
  33.4 0.8 %copy.15 = bf16[64,4096]{1,0:T(8,128)(2,1)} copy(bf16[64,4096]{1,0:T(8,128)(2,1)S(1)} %get-tuple-element.2) | data formatting | bytes 1048576
  34.2 0.6 %copy.16 = bf16[2,4096]{1,0:T(2,128)(2,1)} copy(bf16[2,4096]{1,0:T(2,128)(2,1)S(1)} %get-tuple-element.3) | data formatting | bytes 32768

commit v2 on v1

--- a/solution.py
+++ b/solution.py
@@ -306,6 +306,17 @@
             onward(source, zs, EXTRA)
             send(source, EXTRA, partner, 2)
 
+    def receive_far(d):
+        low = z - d
+
+        @pl.when(low >= 0)
+        def _():
+            pltpu.make_async_copy(far_cq.at[low], far_cq.at[low], far_recv.at[low]).wait()
+
+            @pl.when(z < last)
+            def _():
+                far_copy(low, above).start()
+
     def receive_line(d, i):
         for zs, inside in ((z - d, z - d >= 0), (z + d, z + d < n_z)):
 
@@ -437,7 +448,7 @@
 
             @pl.when(middle & by_line(zs))
             def _():
-                sent(other, 0, 1)
+                sent(other, 0, len(BY_LINE))
 
             sent(other, 2)
         return carry
@@ -446,8 +457,9 @@
 
 
 HEADS = (0, 1, 2, 3)
-MOVED = None
-EXTRA_HEAD = 1
+BY_LINE = (3,)
+LEAD = 2
+AHEAD = 2
 
 
 def pack_rows(values):
@@ -493,6 +505,7 @@
     acc,
     cq,
     far_cq,
+    far_rows,
     part_out,
     part_in,
     lse_out,
@@ -667,6 +680,12 @@
                     jnp.float32
                 )
 
+    for zs in range(last):
+
+        @pl.when(zs >= z)
+        def _():
+            far_cq[zs] = jnp.zeros(far_cq.shape[1:], jnp.bfloat16)
+
     spread(cq)
     q[:, many:, :] = rows16[...].astype(jnp.bfloat16)
     for copy in small[1:]:
@@ -689,10 +708,7 @@
         top = jnp.max(s, axis=1, keepdims=True)
         w = jnp.exp2(s - top)
         row_max[h, many:, :] = jnp.broadcast_to(top, (few, HD))
-        folded = w[:, :HD]
-        for b in range(1, s.shape[1] // HD):
-            folded = folded + w[:, b * HD : (b + 1) * HD]
-        row_sum[h, many:, :] = folded
+        row_sum[h, many:, :] = jnp.broadcast_to(jnp.sum(w, axis=1, keepdims=True), (few, HD))
         acc[h, many:, :] = jnp.dot(
             w.astype(jnp.bfloat16), values, preferred_element_type=jnp.float32
         )
@@ -706,6 +722,9 @@
 
     def plane_rows(zs, h, kind, i):
         return kv[pl.ds(zs * plane, plane), h, kind, i].reshape(span, HD)
+
+    def summed(values):
+        return jnp.concatenate([values, jnp.ones(values.shape, jnp.bfloat16)], axis=1)
 
     def attend(h, zs, mode, bias):
         keys = plane_rows(zs, h, 0, 0)
@@ -713,6 +732,7 @@
         if mode != "cache":
             keys = jnp.concatenate([keys, plane_rows(zs, h, 1, 0)], axis=0)
             values = jnp.concatenate([values, plane_rows(zs, h, 1, 1)], axis=0)
+        values = summed(values)
         cut = (total // 2 + 15) // 16 * 16
         for lo, hi in ((0, cut), (cut, total)):
             s = lax.dot_general(
@@ -733,18 +753,25 @@
             alpha = jnp.exp2(old - new)
             w = [jnp.exp2(b - new) for b in blocks]
             row_max[h, lo:hi, :] = new
-            row_sum[h, lo:hi, :] = row_sum[h, lo:hi, :] * alpha + functools.reduce(jnp.add, w)
             wb = jnp.concatenate([b.astype(jnp.bfloat16) for b in w], axis=1)
-            acc[h, lo:hi, :] = acc[h, lo:hi, :] * alpha + jnp.dot(
-                wb, values, preferred_element_type=jnp.float32
-            )
-
-    def foreign(zs):
-        spread(far_cq.at[zs])
+            mixed = jnp.dot(wb, values, preferred_element_type=jnp.float32)
+            acc[h, lo:hi, :] = acc[h, lo:hi, :] * alpha + mixed[:, :HD]
+            row_sum[h, lo:hi, :] = row_sum[h, lo:hi, :] * alpha + mixed[:, HD:]
+
+    def foreign():
+        for zs in range(last):
+            rows = far_cq.at[zs]
+            for h in range(KVH):
+                for g in range(GROUP):
+                    column = (h * GROUP + g) * HD
+                    first = zs * few + g * conts
+                    far_rows[h, first : first + conts, :] = rows[:, column : column + HD].astype(
+                        jnp.float32
+                    )
         sums = []
         for h in range(KVH):
             s = lax.dot_general(
-                rows16[h].astype(jnp.bfloat16),
+                far_rows[h].astype(jnp.bfloat16),
                 plane_rows(z, h, 1, 0),
                 (((1,), (1,)), ((), ())),
                 preferred_element_type=jnp.float32,
@@ -752,13 +779,20 @@
             s = s * SCALE2
             top = jnp.max(s, axis=1, keepdims=True)
             w = jnp.exp2(s - top)
-            under = jnp.sum(w, axis=1, keepdims=True)
-            mixed = jnp.dot(
-                w.astype(jnp.bfloat16), plane_rows(z, h, 1, 1), preferred_element_type=jnp.float32
+            both = jnp.dot(
+                w.astype(jnp.bfloat16),
+                summed(plane_rows(z, h, 1, 1)),
+                preferred_element_type=jnp.float32,
             )
-            part_out[zs, h * few : (h + 1) * few, :] = mixed / under
-            sums.append(jnp.broadcast_to(top + jnp.log2(under), (few, HD)))
-        lse_out[zs] = pack_rows(jnp.concatenate(sums, axis=0))
+            under = both[:, HD:]
+            mixed = both[:, :HD] / under
+            for zs in range(last):
+                part_out[zs, h * few : (h + 1) * few, :] = mixed[zs * few : (zs + 1) * few, :]
+            sums.append(top + jnp.log2(under))
+        for zs in range(last):
+            lse_out[zs] = pack_rows(
+                jnp.concatenate([level[zs * few : (zs + 1) * few, :] for level in sums], axis=0)
+            )
 
     def part_copies(zs):
         return [
@@ -777,7 +811,6 @@
         for i, ref in enumerate((part_in, lse_in)):
             pltpu.make_async_copy(ref.at[zs], ref.at[zs], part_recv.at[zs, i]).wait()
         tile = lse_in[zs]
-        lane = lax.broadcasted_iota(jnp.int32, (few, HD), 1)
         for h in range(KVH):
             level = unpack_rows(tile, h * few, few)
             old = row_max[h, many:, :]
@@ -785,11 +818,22 @@
             alpha = jnp.exp2(old - new)
             beta = jnp.exp2(level - new)
             row_max[h, many:, :] = new
-            row_sum[h, many:, :] = row_sum[h, many:, :] * alpha + jnp.where(lane == 0, beta, 0.0)
+            row_sum[h, many:, :] = row_sum[h, many:, :] * alpha + beta
             acc[h, many:, :] = (
                 acc[h, many:, :] * alpha + part_in[zs, h * few : (h + 1) * few, :] * beta
             )
 
+    def receive_far(d):
+        low = z - d
+
+        @pl.when(low >= 0)
+        def _():
+            pltpu.make_async_copy(far_cq.at[low], far_cq.at[low], far_recv.at[low]).wait()
+
+            @pl.when(z < last)
+            def _():
+                far_copy(low, above).start()
+
     def receive_line(d, i):
         h = HEADS[i]
         low, high = z - d, z + d
@@ -798,20 +842,13 @@
         def _():
             source = device(low, y, core)
             ref = full(source, h)
-            if i == 0:
-                pltpu.make_async_copy(far_cq.at[low], far_cq.at[low], far_recv.at[low]).wait()
-
-                @pl.when(z < last)
-                def _():
-                    far_copy(low, above).start()
-
             arrived(ref, source, h)
 
             @pl.when(z < last)
             def _():
                 send(ref, source, h, above, 0)
 
-            if h == EXTRA_HEAD:
+            if h in BY_LINE:
 
                 @pl.when(low >= lines)
                 def _():
@@ -820,20 +857,6 @@
             else:
                 send(ref, source, h, across, 1)
             send(ref, source, h, partner, 2)
-            if i == KVH - 1:
-
-                @pl.when(low < lines)
-                def _():
-                    other = device(low, 1 - y, core)
-                    extra = full(other, EXTRA_HEAD)
-                    arrived(extra, other, EXTRA_HEAD)
-
-                    @pl.when(z < last)
-                    def _():
-                        send(extra, other, EXTRA_HEAD, above, 0)
-
-                    send(extra, other, EXTRA_HEAD, partner, 2)
-
         @pl.when(high < n_z)
         def _():
             source = device(high, y, core)
@@ -855,17 +878,18 @@
             arrived(ref, source, h)
             send(ref, source, h, partner, 2)
 
-        if h == EXTRA_HEAD:
-            pl.when((zs <= z) & ((zs == z) | (zs >= lines)))(lambda: take(full(source, h)))
-        else:
-            pl.when(zs <= z)(lambda: take(full(source, h)))
+        pl.when(zs <= z)(lambda: take(full(source, h)))
+        if h in BY_LINE:
+            pl.when((zs < lines) & (zs < z) & (z < last))(
+                lambda: send(full(source, h), source, h, above, 0)
+            )
         pl.when(zs > z)(lambda: take(cached(source, h)))
 
     def receive_own(i):
         h = HEADS[i]
         arrived(full(across, h), across, h)
         send(full(across, h), across, h, partner, 2)
-        if h == EXTRA_HEAD:
+        if h in BY_LINE:
 
             @pl.when((z < last) & (z < lines))
             def _():
@@ -881,45 +905,55 @@
     pltpu.make_async_copy(
         q.at[pl.ds(0, KVH), pl.ds(0, many)], q.at[pl.ds(0, KVH), pl.ds(0, many)], query_sem
     ).wait()
-    receive_own(0)
-    receive_own(1)
+    def receive(t, i):
+        q, r = divmod(i + AHEAD - 1, KVH)
+        receive_line(t + 1 + q, r)
+        q, r = divmod(i + LEAD, KVH)
+        if isinstance(t, int):
+            receive_own(r) if t + q == 0 else receive_y(z_at(t + q), r)
+        else:
+            pl.when(t + q < n_z)(lambda: receive_y(z_at(t + q), r))
+
+    def give(zs):
+        for copy in part_copies(zs):
+            copy.start()
+
+    for j in range(AHEAD - 1):
+        receive_line(1 + j // KVH, j % KVH)
+    for j in range(LEAD):
+        receive_own(j)
     bias = cache_bias(z)
     for i, h in enumerate(HEADS):
+        receive(0, i)
         for yy in (y, 1 - y):
             source = device(z, yy, 1 - core)
             arrived(full(source, h), source, h)
         attend(h, z, "own", bias)
-        receive_line(1, i)
-        if i + 2 < KVH:
-            receive_own(i + 2)
-
-    @pl.when(z > 0)
-    def _():
-        foreign(z - 1)
-
-    def give(zs):
-        for copy in part_copies(zs):
-            copy.start()
+        if i == 0:
+            receive_far(1)
+
+    receive_far(2)
 
     def step(t, carry):
         zs = z_at(t)
         bias = cache_bias(zs)
-        receive_y(zs, 0)
         for i, h in enumerate(HEADS):
-            if i + 1 < KVH:
-                receive_y(zs, i + 1)
+            receive(t, i)
             pair_arrived(zs, i)
             pl.when(zs < z)(lambda: attend(h, zs, "all", bias))
             pl.when(zs > z)(lambda: attend(h, zs, "cache", bias))
-
-            if i == 0:
-                pl.when((t == 1) & (z > 0))(lambda: give(z - 1))
-
-            @pl.when(t < last)
-            def _():
-                receive_line(t + 1, i)
-                if i < 2:
-                    pl.when(z - t - 1 >= 0)(lambda: (foreign, give)[i](z - t - 1))
+            if i > 0:
+
+                @pl.when((t == 1) & (z > 0))
+                def _():
+                    if i == 1:
+                        for d in range(3, n_z):
+                            receive_far(d)
+                    if i == 2:
+                        foreign()
+                    if i == 3:
+                        for d in range(1, n_z):
+                            pl.when(z >= d)(lambda: give(z - d))
 
         return carry
 
@@ -931,7 +965,7 @@
 
     lax.fori_loop(z + 1, n_z, collect, 0)
     for h in range(KVH):
-        mixed = acc[h] / jnp.sum(row_sum[h], axis=1, keepdims=True)
+        mixed = acc[h] / row_sum[h]
         for g in range(GROUP):
             column = (h * GROUP + g) * HD
             out_ref[:, column : column + HD] = mixed[
@@ -973,7 +1007,7 @@
                 sent(source, 0, KVH)
                 pltpu.make_async_copy(far_cq.at[zs], far_cq.at[zs], far_send.at[zs]).wait()
 
-            pl.when(zs < lines)(lambda: sent(source, 1, KVH - 1))
+            pl.when(zs < lines)(lambda: sent(source, 1, KVH - len(BY_LINE)))
             pl.when(zs >= lines)(lambda: sent(source, 1, KVH))
             sent(source, 2, KVH)
             for copy in part_copies(zs):
@@ -989,7 +1023,7 @@
         @pl.when(zs <= z)
         def _():
             sent(other, 2, KVH)
-            pl.when((z < last) & (zs < lines))(lambda: sent(other, 0, 1))
+            pl.when((z < last) & (zs < lines))(lambda: sent(other, 0, len(BY_LINE)))
 
         return carry
 
@@ -1041,6 +1075,7 @@
                 state,
                 pltpu.VMEM(cq.shape, jnp.bfloat16),
                 pltpu.VMEM((n_z,) + cq.shape, jnp.bfloat16),
+                pltpu.VMEM((KVH, few * (n_z - 1), HD), jnp.float32),
                 part,
                 part,
                 levels,

time: 35 us -> 32.5 us (0.929)
  Pallas kernels: 31.5 us -> 29 us
    pallas_call x1, Pallas kernels: 31.5 us -> 29 us  [plane_body(): pl.pallas_call(functools.partial(plane_kernel, n_z), out_shape=(pltpu.VME...]
where the time goes in v2:
time: 32.5 us; the launch traced here: 32.3 us
  Pallas kernels  29 us (89%)
  between operations  1.93 us (6%)
  local copies, waits for them, and re-layouts  1.4 us (4%)
    pallas_call x1, Pallas kernels, plane_body(): pl.pallas_call(functools.partial(plane_kernel, n_z), out_shape=(pltpu.VME...  29 us
    unnamed x2, local copies, waits for them, and re-layouts  1.4 us

profile of v2, /device:TPU:25, one launch (start us, length us, event | category | flops | bytes accessed | tf_op | source)
XLA Modules:
  0.0 32.3 jit_solution(6720595627776104614)
XLA Ops:
  1.9 29.0 %shard_map.122 = (bf16[64,4096]{1,0:T(8,128)(2,1)S(1)}, bf16[2,4096]{1,0:T(2,128)(2,1)S(1)}) custom-call(bf16[64,512]{1,0:T(8,128)(2,1)} %ck_ref.1, bf16[64,512]{1,0:T(8,128)(2,1)} %cv_ref.1, bf16[64,4096]{1,0:T(8,128)(2,1)} %nq_ref.1, bf16[64,512]{1,0:T(8,128)(2,1)} %nk_ref.1, bf16[64,512]{1,0:T(8,128)(2,1)} %nv_ref.1, bf16[2,4096]{1,0:T(2,128)(2,1)} %cq_hbm.1, ...), custom_call_target="tpu_custom_call" | custom-call | tf_op jit(solution)/shard_map/pallas_call | solution.py:1058
  30.9 0.8 %copy.15 = bf16[64,4096]{1,0:T(8,128)(2,1)} copy(bf16[64,4096]{1,0:T(8,128)(2,1)S(1)} %get-tuple-element.2) | data formatting | bytes 1048576
  31.7 0.6 %copy.16 = bf16[2,4096]{1,0:T(2,128)(2,1)} copy(bf16[2,4096]{1,0:T(2,128)(2,1)S(1)} %get-tuple-element.3) | data formatting | bytes 32768

commit v3 on v2

--- a/solution.py
+++ b/solution.py
@@ -550,6 +550,22 @@
     above = device(z + 1, y, core)
     below = device(z - 1, y, core)
 
+    barrier = pltpu.get_barrier_semaphore()
+
+    def greet(target):
+        pl.semaphore_signal(barrier, inc=1, device_id={"ctx": target}, device_id_type=MESH)
+
+    greet(partner)
+    greet(across)
+
+    @pl.when(z > 0)
+    def _():
+        greet(below)
+
+    @pl.when(z < last)
+    def _():
+        greet(above)
+
     for h in HEADS:
         cols = pl.ds(h * HD, HD)
         for kind, pair in enumerate(((ck_ref, cv_ref), (nk_ref, nv_ref))):
@@ -581,22 +597,6 @@
     ]
     for copy in suffix_copies:
         copy.start()
-
-    barrier = pltpu.get_barrier_semaphore()
-
-    def greet(target):
-        pl.semaphore_signal(barrier, inc=1, device_id={"ctx": target}, device_id_type=MESH)
-
-    greet(partner)
-    greet(across)
-
-    @pl.when(z > 0)
-    def _():
-        greet(below)
-
-    @pl.when(z < last)
-    def _():
-        greet(above)
 
     line_neighbours = (z + n_z - 1) // n_z + (2 * n_z - 2 - z) // n_z
     pl.semaphore_wait(barrier, n_y + line_neighbours)

time: 32.5 us -> 32.4 us (level)
  no operation moved by 1% of the time
where the time goes in v3:
time: 32.4 us; the launch traced here: 32.2 us
  Pallas kernels  28.9 us (89%)
  between operations  1.93 us (6%)
  local copies, waits for them, and re-layouts  1.4 us (4%)
    pallas_call x1, Pallas kernels, plane_body(): pl.pallas_call(functools.partial(plane_kernel, n_z), out_shape=(pltpu.VME...  28.9 us
    unnamed x2, local copies, waits for them, and re-layouts  1.4 us

profile of v3, /device:TPU:25, one launch (start us, length us, event | category | flops | bytes accessed | tf_op | source)
XLA Modules:
  0.0 32.2 jit_solution(13352135710229857898)
XLA Ops:
  1.9 28.9 %shard_map.122 = (bf16[64,4096]{1,0:T(8,128)(2,1)S(1)}, bf16[2,4096]{1,0:T(2,128)(2,1)S(1)}) custom-call(bf16[64,512]{1,0:T(8,128)(2,1)} %ck_ref.1, bf16[64,512]{1,0:T(8,128)(2,1)} %cv_ref.1, bf16[64,4096]{1,0:T(8,128)(2,1)} %nq_ref.1, bf16[64,512]{1,0:T(8,128)(2,1)} %nk_ref.1, bf16[64,512]{1,0:T(8,128)(2,1)} %nv_ref.1, bf16[2,4096]{1,0:T(2,128)(2,1)} %cq_hbm.1, ...), custom_call_target="tpu_custom_call" | custom-call | tf_op jit(solution)/shard_map/pallas_call | solution.py:1058
  30.8 0.8 %copy.15 = bf16[64,4096]{1,0:T(8,128)(2,1)} copy(bf16[64,4096]{1,0:T(8,128)(2,1)S(1)} %get-tuple-element.2) | data formatting | bytes 1048576
  31.6 0.6 %copy.16 = bf16[2,4096]{1,0:T(2,128)(2,1)} copy(bf16[2,4096]{1,0:T(2,128)(2,1)S(1)} %get-tuple-element.3) | data formatting | bytes 32768

commit v4 on v3

--- a/solution.py
+++ b/solution.py
@@ -584,13 +584,6 @@
     ]
     for copy in small:
         copy.start()
-    for h in HEADS:
-        for g in range(GROUP):
-            pltpu.make_async_copy(
-                nq_ref.at[:, pl.ds((h * GROUP + g) * HD, HD)],
-                q.at[h, pl.ds(g * prompt_rows, prompt_rows)],
-                query_sem,
-            ).start()
     suffix_copies = [
         pltpu.make_async_copy(sk_ref, sk, suffix_sem.at[0]),
         pltpu.make_async_copy(sv_ref, sv, suffix_sem.at[1]),
@@ -658,6 +651,13 @@
 
         send(full(me, h), me, h, partner, 2)
 
+    for h in HEADS:
+        for g in range(GROUP):
+            pltpu.make_async_copy(
+                nq_ref.at[:, pl.ds((h * GROUP + g) * HD, HD)],
+                q.at[h, pl.ds(g * prompt_rows, prompt_rows)],
+                query_sem,
+            ).start()
     near = jnp.minimum(z, last - z)
 
     def z_at(t):

time: 32.4 us -> 32.4 us (level)
  no operation moved by 1% of the time
where the time goes in v4:
time: 32.4 us; the launch traced here: 32.2 us
  Pallas kernels  28.9 us (89%)
  between operations  1.93 us (6%)
  local copies, waits for them, and re-layouts  1.4 us (4%)
    pallas_call x1, Pallas kernels, plane_body(): pl.pallas_call(functools.partial(plane_kernel, n_z), out_shape=(pltpu.VME...  28.9 us
    unnamed x2, local copies, waits for them, and re-layouts  1.4 us

profile of v4, /device:TPU:25, one launch (start us, length us, event | category | flops | bytes accessed | tf_op | source)
XLA Modules:
  0.0 32.2 jit_solution(17180109978127084169)
XLA Ops:
  1.9 28.9 %shard_map.122 = (bf16[64,4096]{1,0:T(8,128)(2,1)S(1)}, bf16[2,4096]{1,0:T(2,128)(2,1)S(1)}) custom-call(bf16[64,512]{1,0:T(8,128)(2,1)} %ck_ref.1, bf16[64,512]{1,0:T(8,128)(2,1)} %cv_ref.1, bf16[64,4096]{1,0:T(8,128)(2,1)} %nq_ref.1, bf16[64,512]{1,0:T(8,128)(2,1)} %nk_ref.1, bf16[64,512]{1,0:T(8,128)(2,1)} %nv_ref.1, bf16[2,4096]{1,0:T(2,128)(2,1)} %cq_hbm.1, ...), custom_call_target="tpu_custom_call" | custom-call | tf_op jit(solution)/shard_map/pallas_call | solution.py:1058
  30.8 0.8 %copy.15 = bf16[64,4096]{1,0:T(8,128)(2,1)} copy(bf16[64,4096]{1,0:T(8,128)(2,1)S(1)} %get-tuple-element.2) | data formatting | bytes 1048576
  31.6 0.6 %copy.16 = bf16[2,4096]{1,0:T(2,128)(2,1)} copy(bf16[2,4096]{1,0:T(2,128)(2,1)S(1)} %get-tuple-element.3) | data formatting | bytes 32768

commit v5 on v4

--- a/solution.py
+++ b/solution.py
@@ -623,6 +623,21 @@
             device_id_type=MESH,
         )
 
+    for h in HEADS:
+        pltpu.make_async_copy(full(me, h), full(me, h), local_sem.at[h]).wait()
+
+        @pl.when(z < last)
+        def _():
+            send(full(me, h), me, h, above, 0)
+
+        send(full(me, h), me, h, across, 1)
+
+        @pl.when(z > 0)
+        def _():
+            send(cached(me, h), me, h, below, 3)
+
+        send(full(me, h), me, h, partner, 2)
+
     small[0].wait()
 
     @pl.when(z < last)
@@ -635,21 +650,6 @@
             device_id={"ctx": above},
             device_id_type=MESH,
         ).start()
-
-    for h in HEADS:
-        pltpu.make_async_copy(full(me, h), full(me, h), local_sem.at[h]).wait()
-
-        @pl.when(z < last)
-        def _():
-            send(full(me, h), me, h, above, 0)
-
-        send(full(me, h), me, h, across, 1)
-
-        @pl.when(z > 0)
-        def _():
-            send(cached(me, h), me, h, below, 3)
-
-        send(full(me, h), me, h, partner, 2)
 
     for h in HEADS:
         for g in range(GROUP):

time: 32.4 us -> 32.4 us (level)
  no operation moved by 1% of the time
where the time goes in v5:
time: 32.4 us; the launch traced here: 32.2 us
  Pallas kernels  28.9 us (89%)
  between operations  1.93 us (6%)
  local copies, waits for them, and re-layouts  1.4 us (4%)
    pallas_call x1, Pallas kernels, plane_body(): pl.pallas_call(functools.partial(plane_kernel, n_z), out_shape=(pltpu.VME...  28.9 us
    unnamed x2, local copies, waits for them, and re-layouts  1.4 us

profile of v5, /device:TPU:25, one launch (start us, length us, event | category | flops | bytes accessed | tf_op | source)
XLA Modules:
  0.0 32.2 jit_solution(15578615393096492871)
XLA Ops:
  1.9 28.9 %shard_map.122 = (bf16[64,4096]{1,0:T(8,128)(2,1)S(1)}, bf16[2,4096]{1,0:T(2,128)(2,1)S(1)}) custom-call(bf16[64,512]{1,0:T(8,128)(2,1)} %ck_ref.1, bf16[64,512]{1,0:T(8,128)(2,1)} %cv_ref.1, bf16[64,4096]{1,0:T(8,128)(2,1)} %nq_ref.1, bf16[64,512]{1,0:T(8,128)(2,1)} %nk_ref.1, bf16[64,512]{1,0:T(8,128)(2,1)} %nv_ref.1, bf16[2,4096]{1,0:T(2,128)(2,1)} %cq_hbm.1, ...), custom_call_target="tpu_custom_call" | custom-call | tf_op jit(solution)/shard_map/pallas_call | solution.py:1058
  30.8 0.8 %copy.15 = bf16[64,4096]{1,0:T(8,128)(2,1)} copy(bf16[64,4096]{1,0:T(8,128)(2,1)S(1)} %get-tuple-element.2) | data formatting | bytes 1048576
  31.6 0.6 %copy.16 = bf16[2,4096]{1,0:T(2,128)(2,1)} copy(bf16[2,4096]{1,0:T(2,128)(2,1)S(1)} %get-tuple-element.3) | data formatting | bytes 32768
